TPU v7x, 128 devices: a whole 4x4x4 slice. The times are simulated.
128 devices in a mesh: edp: 2 (over y_hi), ep: 64 (over y_lo, z, x, core).
Axes of the slice: x: 4, y: 4 (y_hi: 2, y_lo: 2; y = y_hi * 2 + y_lo), z: 4, core: 2. Of those that a mesh axis runs over, the one named last changes fastest.
Arguments:
- tokens: bfloat16 [16384, 2048], P(('edp', 'ep')), may hold values from -6 to 6
- routes: int32 [16384, 8], P(('edp', 'ep')), may hold values from 0 to 63, all different within a row; in each aligned block of 128 rows (0 to 127, 128 to 255, ...) at most 24 rows name the same one
- gate_weights: float32 [16384, 8], P(('edp', 'ep')), may hold values from 0.05 to 0.5
- w_gate: bfloat16 [64, 2048, 768], P('ep'), may hold values from -0.125 to 0.125
- w_up: bfloat16 [64, 2048, 768], P('ep'), may hold values from -0.125 to 0.125
- w_down: bfloat16 [64, 768, 2048], P('ep'), may hold values from -0.21875 to 0.21875
- saved_inputs: bfloat16 [64, 512, 2048], P('ep', 'edp'), may hold values from -6 to 6
- saved_cotangent: bfloat16 [64, 512, 2048], P('ep', 'edp'), may hold values from -0.59765625 to 0.59765625
Outputs:
- mixed: bfloat16 [16384, 2048], P(('edp', 'ep'))
- grad_gate: float32 [64, 2048, 768], P('ep', 'edp')
- grad_up: float32 [64, 2048, 768], P('ep', 'edp')
- grad_down: float32 [64, 768, 2048], P('ep', 'edp')
Inputs may be any that keep to these rules, and one draw needn't show every extreme that they name: `routes`: each token names 8 different experts. In each aligned block of 128 tokens (the tokens of one device) no expert is named more than 24 times, a bound that some block reaches in every draw.
All inputs are finite; a program needn't handle non-finite values.
Results may differ from a plain program's by a relative error of at most 0.006.
Values may be sent and summed in bfloat16 or wider, within the bound.
No kernel may reach another device: no remote copies, remote signals or barrier semaphores. Data moves between devices by JAX's collectives and lax.ppermute only.
A program may use at most 128 MiB of HBM per device.

v0:
```python
import jax
import jax.numpy as jnp
from jax import lax
from jax.sharding import PartitionSpec as P


def side_by_side(arrays, axis, dim, along):
    widths = [a.shape[along] for a in arrays]
    both = jnp.concatenate(arrays, axis=along)
    result = lax.all_gather(both, axis, axis=dim, tiled=True)
    return tuple(jnp.split(result, [sum(widths[:k]) for k in range(1, len(widths))], axis=along))


def expert_mlp(row_data, w_gate, w_up, w_down):
    gate_pre = jnp.dot(row_data, w_gate, preferred_element_type=jnp.float32)
    up_pre = jnp.dot(row_data, w_up, preferred_element_type=jnp.float32)
    hidden = (jax.nn.silu(gate_pre) * up_pre).astype(jnp.bfloat16)
    return jnp.dot(hidden, w_down, preferred_element_type=jnp.float32).astype(jnp.bfloat16)


def expert_grads(inputs, cotangent, w_gate, w_up, w_down):
    gate_pre = jnp.dot(inputs, w_gate, preferred_element_type=jnp.float32)
    up_pre = jnp.dot(inputs, w_up, preferred_element_type=jnp.float32)
    activated = jax.nn.silu(gate_pre)
    hidden = (activated * up_pre).astype(jnp.bfloat16)
    d_hidden = jnp.einsum("rd,fd->rf", cotangent, w_down, preferred_element_type=jnp.float32)
    sigmoid_gate = jax.nn.sigmoid(gate_pre)
    d_gate = (d_hidden * up_pre * sigmoid_gate * (1.0 + gate_pre * (1.0 - sigmoid_gate))).astype(
        jnp.bfloat16
    )
    d_up = (d_hidden * activated).astype(jnp.bfloat16)
    return (hidden, d_gate, d_up)


def rounded(value):
    return lax.optimization_barrier(value.astype(jnp.bfloat16)).astype(jnp.float32)


def dispatch_plan(routes, experts, capacity):
    route_flat = routes.reshape(-1)
    one_hot = (route_flat[:, None] == jnp.arange(experts, dtype=jnp.int32)[None, :]).astype(
        jnp.int32
    )
    running = jnp.cumsum(one_hot, axis=0) - 1
    slot_index = jnp.sum(running * one_hot, axis=1)
    return route_flat * capacity + slot_index


def shards(tokens, routes, gate_weights, w_gate, w_up, w_down, saved_inputs, saved_cotangent):
    experts = lax.axis_size("ep")
    tok_rows, width = tokens.shape
    top_count = routes.shape[1]
    capacity = 3 * tok_rows * top_count // (2 * experts)
    position = dispatch_plan(routes, experts, capacity)
    send_buffer = jnp.zeros((experts * capacity, width), jnp.bfloat16)
    send_buffer = send_buffer.at[position].set(jnp.repeat(tokens, top_count, axis=0))
    send_buffer = send_buffer.reshape(experts, capacity, width)
    gate_mat, up_mat, down_mat = (w_gate[0], w_up[0], w_down[0])
    received = lax.all_to_all(send_buffer, "ep", split_axis=0, concat_axis=0, tiled=True)
    output = expert_mlp(received.reshape(-1, width), gate_mat, up_mat, down_mat)
    returned = lax.all_to_all(
        output.reshape(received.shape), "ep", split_axis=0, concat_axis=0, tiled=True
    )
    picked = returned.reshape(experts * capacity, width)[position]
    weighted = (
        picked.astype(jnp.float32).reshape(tok_rows, top_count, width) * gate_weights[:, :, None]
    )
    combined = jnp.sum(weighted, axis=1).astype(jnp.bfloat16)
    all_inputs, all_cotangent = side_by_side((saved_inputs, saved_cotangent), "edp", 1, 0)
    replicas = lax.axis_size("edp")
    own_index = lax.axis_index("edp")
    row_block = saved_inputs.shape[1]
    half_width = width // replicas
    half_hidden = gate_mat.shape[1] // replicas
    grad_g = jnp.zeros((half_width, gate_mat.shape[1]), jnp.float32)
    grad_u = jnp.zeros((half_width, gate_mat.shape[1]), jnp.float32)
    grad_d = jnp.zeros((half_hidden, width), jnp.float32)
    for replica in range(replicas):
        inputs = all_inputs[0, replica * row_block : (replica + 1) * row_block]
        cotangent = all_cotangent[0, replica * row_block : (replica + 1) * row_block]
        hidden, d_gate, d_up = expert_grads(inputs, cotangent, gate_mat, up_mat, down_mat)
        in_cols = lax.dynamic_slice_in_dim(inputs, own_index * half_width, half_width, 1)
        hidden_cols = lax.dynamic_slice_in_dim(hidden, own_index * half_hidden, half_hidden, 1)
        grad_g = grad_g + rounded(
            jnp.einsum("rd,rf->df", in_cols, d_gate, preferred_element_type=jnp.float32)
        )
        grad_u = grad_u + rounded(
            jnp.einsum("rd,rf->df", in_cols, d_up, preferred_element_type=jnp.float32)
        )
        grad_d = grad_d + rounded(
            jnp.einsum("rf,rd->fd", hidden_cols, cotangent, preferred_element_type=jnp.float32)
        )
    grad_gate, grad_up, grad_down = (grad_g[None], grad_u[None], grad_d[None])
    return (combined, grad_gate, grad_up, grad_down)


def solution(mesh):
    return jax.shard_map(
        shards,
        mesh=mesh,
        in_specs=(
            P(("edp", "ep"), None),
            P(("edp", "ep"), None),
            P(("edp", "ep"), None),
            P("ep", None, None),
            P("ep", None, None),
            P("ep", None, None),
            P("ep", "edp", None),
            P("ep", "edp", None),
        ),
        out_specs=(
            P(("edp", "ep"), None),
            P("ep", "edp", None),
            P("ep", "edp", None),
            P("ep", "edp", None),
        ),
        check_vma=False,
    )
```

profile of v0, /device:TPU:66, one launch (start us, length us, event | category | flops | bytes accessed | tf_op | source)
XLA Modules:
  0.0 293.9 jit_solution(12249136791004862306)
XLA Ops:
  7.2 0.0 copy-start
  7.2 0.8 broadcast_multiply_fusion
  8.0 0.9 copy.14
  8.9 0.1 eq.29
  9.0 0.1 eq.25
  9.1 0.1 copy.13
  9.2 0.1 mul.87
  9.3 0.7 fusion.41
  10.0 31.1 %reduce-window.6 = s32[64,8,128]{2,1,0:T(8,128)S(1)} reduce-window(s32[64,8,128]{2,1,0:T(8,128)} %fusion.41, s32[]{:T(128)} %constant.11.clone.1), window={size=1x1x128 pad=0_0x0_0x127_0}, to_apply=%region_0.0 | reduce-window | flops 8323072 | bytes 524292 | tf_op jit(solution)/shard_map/reduce-window
  41.1 0.8 slice.30
  42.0 1.1 copy.16
  43.1 0.1 copy.17
  43.2 0.1 add_add_fusion
  43.3 0.1 fusion.40
  43.4 10.7 %scatter_custom_fusion = bf16[1536,2048]{1,0:T(8,128)(2,1)} fusion(s32[1024]{0:T(1024)S(1)} %bitcast.97, bf16[]{:T(256)} %constant.13.clone.1, bf16[128,2048]{1,0:T(8,128)(2,1)} %param.8), kind=kCustom, calls=%fused_computation.6 | custom fusion | bytes 6815746 | tf_op jit(solution)/shard_map/scatter | solution.py:56
  54.0 9.1 %all-to-all-start = ((bf16[64,24,2048]{2,1,0:T(8,128)(2,1)}), bf16[64,24,2048]{2,1,0:T(8,128)(2,1)}, u32[]{:S(2)}, u32[]{:S(2)}) async-start(bf16[64,24,2048]{2,1,0:T(8,128)(2,1)} %bitcast.92), calls=%async_computation | async-start | bytes 12582912 | tf_op jit(solution)/shard_map/all_to_all | solution.py:59
  63.2 0.2 all-gather.2.cloned.1.call-start
  63.4 3.1 %pad_maximum_fusion = bf16[2,256,2048]{2,1,0:T(8,128)(2,1)} fusion(bf16[1,256,2048]{2,1,0:T(8,128)(2,1)} %param.15, bf16[1,256,2048]{2,1,0:T(8,128)(2,1)} %param.14), kind=kLoop, calls=%fused_computation.30 | loop fusion | flops 1048576 | bytes 4194304 | tf_op jit(solution)/shard_map/concatenate | solution.py:9
  66.5 0.0 all-gather.2.cloned.1.call-update
  66.5 90.5 %all-to-all-done = bf16[64,24,2048]{2,1,0:T(8,128)(2,1)} async-done(((bf16[64,24,2048]{2,1,0:T(8,128)(2,1)}), bf16[64,24,2048]{2,1,0:T(8,128)(2,1)}, u32[]{:S(2)}, u32[]{:S(2)}) %all-to-all-start) | async-done | bytes 6291488 | tf_op jit(solution)/shard_map/all_to_all | solution.py:59
  157.0 8.2 %fusion.17 = f32[1536,768]{1,0:T(8,128)S(1)} fusion(bf16[1536,2048]{1,0:T(8,128)(2,1)} %bitcast.6, bf16[1,2048,768]{2,1,0:T(8,128)(2,1)} %param.11), kind=kOutput, calls=%fused_computation.22 | convolution fusion | flops 4831838208 | bytes 14155776 | tf_op jit(solution)/shard_map/dot_general | solution.py:15
  165.3 7.5 %multiply_convert_fusion = bf16[1536,768]{1,0:T(8,128)(2,1)S(1)} fusion(f32[1536,768]{1,0:T(8,128)S(1)} %fusion.17, bf16[1536,2048]{1,0:T(8,128)(2,1)} %bitcast.6, bf16[1,2048,768]{2,1,0:T(8,128)(2,1)S(1)} %copy-done.4), kind=kOutput, calls=%fused_computation.5 | convolution fusion | flops 4838916096 | bytes 16515072 | tf_op jit(solution)/shard_map/dot_general | solution.py:16
  172.8 7.0 %convolution_convert_fusion = bf16[1536,2048]{1,0:T(8,128)(2,1)} fusion(bf16[1536,768]{1,0:T(8,128)(2,1)S(1)} %multiply_convert_fusion, bf16[1,768,2048]{2,1,0:T(8,128)(2,1)S(1)} %copy-done), kind=kOutput, calls=%fused_computation.4 | convolution fusion | flops 4834983936 | bytes 11796480 | tf_op jit(solution)/shard_map/dot_general | solution.py:18
  179.9 6.8 %all-to-all-start.1 = ((bf16[64,24,2048]{2,1,0:T(8,128)(2,1)}), bf16[64,24,2048]{2,1,0:T(8,128)(2,1)}, u32[]{:S(2)}, u32[]{:S(2)}) async-start(bf16[64,24,2048]{2,1,0:T(8,128)(2,1)} %bitcast.93), calls=%async_computation.1 | async-start | bytes 12582912 | tf_op jit(solution)/shard_map/all_to_all | solution.py:61
  186.7 0.1 copy.18
  186.8 2.8 all-gather.2.cloned.1.call-done
  189.6 2.4 fusion.3
  192.0 0.1 copy-done.1
  192.1 3.0 %fusion.25 = (f32[256,768]{1,0:T(8,128)S(1)}, f32[256,768]{1,0:T(8,128)S(1)}) fusion(bf16[1,2048,768]{2,1,0:T(8,128)(2,1)} %param.11, bf16[2,512,2048]{2,1,0:T(8,128)(2,1)S(1)} %copy-done.1), kind=kOutput, calls=%fused_computation.46 | convolution fusion | flops 806092800 | bytes 5767168 | tf_op jit(solution)/shard_map/dot_general | solution.py:22
  195.1 0.2 fusion.58
  195.3 0.7 convolution_convert_fusion.3
  196.0 0.0 copy-start.3
  196.0 1.0 fusion.5
  197.1 0.9 copy-done.3
  197.9 1.1 fusion.26
  199.0 0.7 convolution_convert_fusion.4
  199.7 1.2 copy-done.5
  200.9 1.0 fusion.8
  201.9 0.8 convolution_convert_fusion.5
  202.6 1.0 fusion.10
  203.6 0.8 convolution_convert_fusion.6
  204.4 0.6 convolution_convert_fusion.1
  205.1 0.6 convolution_convert_fusion.2
  205.7 3.4 %add_bitcast_fusion.1 = (f32[1,1024,768]{2,1,0:T(8,128)}, f32[1,1024,768]{2,1,0:T(8,128)}) fusion(bf16[1024,768]{1,0:T(8,128)(2,1)S(1)} %convolution_convert_fusion.3, bf16[1024,768]{1,0:T(8,128)(2,1)S(1)} %convolution_convert_fusion.4, bf16[1024,768]{1,0:T(8,128)(2,1)S(1)} %convolution_convert_fusion.5, bf16[1024,768]{1,0:T(8,128)(2,1)S(1)} %convolution_convert_fusion.6), kind=kLoop, calls=%fused_computation.25 | loop fusion | flops 4718592 | bytes 12582912 | tf_op jit(solution)/shard_map/broadcast_in_dim | solution.py:93
  209.1 2.3 add_bitcast_fusion
  211.4 55.7 %all-to-all-done.1 = bf16[64,24,2048]{2,1,0:T(8,128)(2,1)} async-done(((bf16[64,24,2048]{2,1,0:T(8,128)(2,1)}), bf16[64,24,2048]{2,1,0:T(8,128)(2,1)}, u32[]{:S(2)}, u32[]{:S(2)}) %all-to-all-start.1) | async-done | bytes 6291488 | tf_op jit(solution)/shard_map/all_to_all | solution.py:61
  267.1 12.7 %gather_fusion = bf16[1024,2048]{1,0:T(8,128)(2,1)} fusion(bf16[1536,2048]{1,0:T(8,128)(2,1)} %bitcast.11, s32[1024]{0:T(1024)S(1)} %broadcast_clamp_fusion), kind=kCustom, calls=%fused_computation | custom fusion | bytes 8392704 | tf_op jit(solution)/shard_map/gather | solution.py:64
  279.7 7.3 %fusion = bf16[128,2048]{1,0:T(8,128)(2,1)} fusion(bf16[1024,2048]{1,0:T(8,128)(2,1)} %gather_fusion, f32[128,8]{1,0:T(8,128)S(1)} %copy.18), kind=kLoop, calls=%fused_computation.3 | loop fusion | flops 6029312 | bytes 4722688 | tf_op jit(solution)/shard_map/reduce_sum | solution.py:68
  (11 shorter events, 0.1 us)
Async XLA Ops:
  7.2 165.6 %copy-start = (bf16[1,768,2048]{2,1,0:T(8,128)(2,1)S(1)}, bf16[1,768,2048]{2,1,0:T(8,128)(2,1)}, u32[]{:S(2)}) copy-start(bf16[1,768,2048]{2,1,0:T(8,128)(2,1)} %param.13) | copy-start | bytes 9437188
  54.0 103.0 %all-to-all-start = ((bf16[64,24,2048]{2,1,0:T(8,128)(2,1)}), bf16[64,24,2048]{2,1,0:T(8,128)(2,1)}, u32[]{:S(2)}, u32[]{:S(2)}) async-start(bf16[64,24,2048]{2,1,0:T(8,128)(2,1)} %bitcast.92), calls=%async_computation | async-start | bytes 12582912 | tf_op jit(solution)/shard_map/all_to_all | solution.py:59
  63.2 126.4 %all-gather.2.cloned.1.call-start = ((), (), s32[]{:S(2)}) async-start(), calls=%async_computation.2 | async-start | bytes 6291456 | tf_op jit(solution)/shard_map/all_gather | solution.py:10
  157.0 8.2 %copy-start.4 = (bf16[1,2048,768]{2,1,0:T(8,128)(2,1)S(1)}, bf16[1,2048,768]{2,1,0:T(8,128)(2,1)}, u32[]{:S(2)}) copy-start(bf16[1,2048,768]{2,1,0:T(8,128)(2,1)} %param.12) | copy-start | bytes 9437188
  179.9 6.8 %copy-start.2 = (f32[128,8]{0,1:T(8,128)S(1)}, f32[128,8]{0,1:T(8,128)}, u32[]{:S(2)}) copy-start(f32[128,8]{0,1:T(8,128)} %param.10) | copy-start | bytes 12292
  179.9 87.2 %all-to-all-start.1 = ((bf16[64,24,2048]{2,1,0:T(8,128)(2,1)}), bf16[64,24,2048]{2,1,0:T(8,128)(2,1)}, u32[]{:S(2)}, u32[]{:S(2)}) async-start(bf16[64,24,2048]{2,1,0:T(8,128)(2,1)} %bitcast.93), calls=%async_computation.1 | async-start | bytes 12582912 | tf_op jit(solution)/shard_map/all_to_all | solution.py:61
  189.6 2.5 copy-start.1
  196.0 1.9 copy-start.3
  199.0 1.9 copy-start.5
Sparse Core Ops, SparseCore 0:
  66.6 122.9 all-gather.1
where the time goes:
time: 299 us; the launch traced here: 294 us
  waiting for transfers between devices  149 us (50%)
  other arithmetic  48.9 us (16%)
  matrix products  36.3 us (12%)
  local copies, waits for them, and re-layouts  29.1 us (10%)
  starting transfers between devices  16.2 us (5%)
  between operations  14.3 us (5%)
    all_to_all x1, waiting for transfers between devices, shards(): lax.all_to_all(send_buffer, 'ep', split_axis=0, concat_axis=0, tiled=True)  90.5 us
    all_to_all x1, waiting for transfers between devices, shards(): lax.all_to_all(output.reshape(received.shape), 'ep', split_axis=0, concat...  55.7 us
    another operation x2, other arithmetic  31.1 us
    gather x1, local copies, waits for them, and re-layouts, shards(): picked = returned.reshape(experts * capacity, width)[position]  12.7 us
    scatter x1, local copies, waits for them, and re-layouts, shards(): send_buffer.at[position].set(jnp.repeat(tokens, top_count, axis=0))  10.7 us
    all_to_all x1, starting transfers between devices, shards(): lax.all_to_all(send_buffer, 'ep', split_axis=0, concat_axis=0, tiled=True)  9.14 us
    dot_general x1, matrix products, expert_mlp(): gate_pre = jnp.dot(row_data, w_gate, preferred_element_type=jnp.float32)  8.21 us
    dot_general x1, matrix products, expert_mlp(): up_pre = jnp.dot(row_data, w_up, preferred_element_type=jnp.float32)  7.52 us
  transfers between devices with their start and end apart: 3, of which 3 were waited for; matrix products, arithmetic and copies ran while one was open for 15% of the time, Pallas kernels for 0%

commit v1 on v0

--- a/solution.py
+++ b/solution.py
@@ -2,13 +2,6 @@
 import jax.numpy as jnp
 from jax import lax
 from jax.sharding import PartitionSpec as P
-
-
-def side_by_side(arrays, axis, dim, along):
-    widths = [a.shape[along] for a in arrays]
-    both = jnp.concatenate(arrays, axis=along)
-    result = lax.all_gather(both, axis, axis=dim, tiled=True)
-    return tuple(jnp.split(result, [sum(widths[:k]) for k in range(1, len(widths))], axis=along))
 
 
 def expert_mlp(row_data, w_gate, w_up, w_down):
@@ -36,14 +29,47 @@
     return lax.optimization_barrier(value.astype(jnp.bfloat16)).astype(jnp.float32)
 
 
-def dispatch_plan(routes, experts, capacity):
-    route_flat = routes.reshape(-1)
-    one_hot = (route_flat[:, None] == jnp.arange(experts, dtype=jnp.int32)[None, :]).astype(
-        jnp.int32
+def slot_table(routes, experts):
+    named = jnp.any(
+        routes[:, :, None] == jnp.arange(experts, dtype=jnp.int32)[None, None, :], axis=1
     )
-    running = jnp.cumsum(one_hot, axis=0) - 1
-    slot_index = jnp.sum(running * one_hot, axis=1)
-    return route_flat * capacity + slot_index
+    rows = routes.shape[0]
+    earlier = (
+        lax.broadcasted_iota(jnp.int32, (rows, rows), 1)
+        < lax.broadcasted_iota(jnp.int32, (rows, rows), 0)
+    ).astype(jnp.bfloat16)
+    before = jnp.dot(earlier, named.astype(jnp.bfloat16), preferred_element_type=jnp.float32)
+    return jnp.where(named, before.astype(jnp.int32), -1)
+
+
+def select_rows(slots, capacity, tokens):
+    rows, experts = slots.shape
+    chosen = slots.T[:, None, :] == jnp.arange(capacity, dtype=jnp.int32)[None, :, None]
+    chosen = chosen.astype(jnp.bfloat16).reshape(experts * capacity, rows)
+    return jnp.dot(chosen, tokens, preferred_element_type=jnp.float32).astype(jnp.bfloat16)
+
+
+def combine_rows(slots, routes, gate_weights, capacity, returned):
+    rows, experts = slots.shape
+    weight = jnp.sum(
+        jnp.where(
+            routes[:, :, None] == jnp.arange(experts, dtype=jnp.int32)[None, None, :],
+            gate_weights[:, :, None],
+            0.0,
+        ),
+        axis=1,
+    )
+    high = lax.reduce_precision(weight, 8, 7)
+    low = weight - high
+    both = jnp.concatenate([high, low], axis=0).astype(jnp.bfloat16)
+    place = jnp.concatenate([slots, slots], axis=0)
+    spread = jnp.where(
+        place[:, :, None] == jnp.arange(capacity, dtype=jnp.int32)[None, None, :],
+        both[:, :, None],
+        jnp.bfloat16(0.0),
+    ).reshape(2 * rows, experts * capacity)
+    halves = jnp.dot(spread, returned, preferred_element_type=jnp.float32)
+    return halves[:rows] + halves[rows:]
 
 
 def shards(tokens, routes, gate_weights, w_gate, w_up, w_down, saved_inputs, saved_cotangent):
@@ -51,33 +77,27 @@
     tok_rows, width = tokens.shape
     top_count = routes.shape[1]
     capacity = 3 * tok_rows * top_count // (2 * experts)
-    position = dispatch_plan(routes, experts, capacity)
-    send_buffer = jnp.zeros((experts * capacity, width), jnp.bfloat16)
-    send_buffer = send_buffer.at[position].set(jnp.repeat(tokens, top_count, axis=0))
-    send_buffer = send_buffer.reshape(experts, capacity, width)
     gate_mat, up_mat, down_mat = (w_gate[0], w_up[0], w_down[0])
+    replicas = lax.axis_size("edp")
+    ring = [(r, (r + 1) % replicas) for r in range(replicas)]
+
+    slots = slot_table(routes, experts)
+    send_buffer = select_rows(slots, capacity, tokens).reshape(experts, capacity, width)
     received = lax.all_to_all(send_buffer, "ep", split_axis=0, concat_axis=0, tiled=True)
     output = expert_mlp(received.reshape(-1, width), gate_mat, up_mat, down_mat)
     returned = lax.all_to_all(
         output.reshape(received.shape), "ep", split_axis=0, concat_axis=0, tiled=True
-    )
-    picked = returned.reshape(experts * capacity, width)[position]
-    weighted = (
-        picked.astype(jnp.float32).reshape(tok_rows, top_count, width) * gate_weights[:, :, None]
-    )
-    combined = jnp.sum(weighted, axis=1).astype(jnp.bfloat16)
-    all_inputs, all_cotangent = side_by_side((saved_inputs, saved_cotangent), "edp", 1, 0)
-    replicas = lax.axis_size("edp")
+    ).reshape(experts * capacity, width)
+    combined = combine_rows(slots, routes, gate_weights, capacity, returned).astype(jnp.bfloat16)
+
     own_index = lax.axis_index("edp")
-    row_block = saved_inputs.shape[1]
     half_width = width // replicas
     half_hidden = gate_mat.shape[1] // replicas
     grad_g = jnp.zeros((half_width, gate_mat.shape[1]), jnp.float32)
     grad_u = jnp.zeros((half_width, gate_mat.shape[1]), jnp.float32)
     grad_d = jnp.zeros((half_hidden, width), jnp.float32)
+    inputs, cotangent = saved_inputs[0], saved_cotangent[0]
     for replica in range(replicas):
-        inputs = all_inputs[0, replica * row_block : (replica + 1) * row_block]
-        cotangent = all_cotangent[0, replica * row_block : (replica + 1) * row_block]
         hidden, d_gate, d_up = expert_grads(inputs, cotangent, gate_mat, up_mat, down_mat)
         in_cols = lax.dynamic_slice_in_dim(inputs, own_index * half_width, half_width, 1)
         hidden_cols = lax.dynamic_slice_in_dim(hidden, own_index * half_hidden, half_hidden, 1)
@@ -90,6 +110,9 @@
         grad_d = grad_d + rounded(
             jnp.einsum("rf,rd->fd", hidden_cols, cotangent, preferred_element_type=jnp.float32)
         )
+        if replica + 1 < replicas:
+            inputs = lax.ppermute(inputs, "edp", ring)
+            cotangent = lax.ppermute(cotangent, "edp", ring)
     grad_gate, grad_up, grad_down = (grad_g[None], grad_u[None], grad_d[None])
     return (combined, grad_gate, grad_up, grad_down)
 

time: 299 us -> 269 us (0.90); the launches traced: 294 us -> 269 us
  blocking collectives: 0 us -> 81.4 us
  other arithmetic: 48.9 us -> 7.79 us
  waiting for transfers between devices: 149 us -> 116 us
  local copies, waits for them, and re-layouts: 29.1 us -> 1.61 us
  matrix products: 36.3 us -> 49.9 us
  between operations: 14.3 us -> 0.9 us
  starting transfers between devices: 16.2 us -> 11 us
    ppermute x0 -> x2, waiting for transfers between devices: none -> 116 us  [the longest x1 116 us: shards(): cotangent = lax.ppermute(cotangent, 'edp', ring)]
    all_to_all x1 -> x0, waiting for transfers between devices: 90.5 us -> none  [shards(): lax.all_to_all(send_buffer, 'ep', split_axis=0, concat_axis=0, tiled=True)]
    all_to_all x0 -> x1, blocking collectives: none -> 81.4 us  [shards(): lax.all_to_all(send_buffer, 'ep', split_axis=0, concat_axis=0, tiled=True)]
    all_to_all x1, waiting for transfers between devices: 55.7 us -> 0.01 us  [shards(): lax.all_to_all(output.reshape(received.shape), 'ep', split_axis=0, concat...]
    another operation x2 -> x1, other arithmetic: 31.1 us -> 0.01 us
    dot_general x0 -> x3, matrix products: none -> 13.3 us  [the longest x1 10.3 us: combine_rows(): halves = jnp.dot(spread, returned, preferred_element_type=jnp.float32)]
    gather x1 -> x0, local copies, waits for them, and re-layouts: 12.7 us -> none  [shards(): picked = returned.reshape(experts * capacity, width)[position]]
    scatter x1 -> x0, local copies, waits for them, and re-layouts: 10.7 us -> none  [shards(): send_buffer.at[position].set(jnp.repeat(tokens, top_count, axis=0))]
  transfers between devices with their start and end apart: 3 -> 3, of which waited for: 3 -> 1; matrix products, arithmetic and copies ran while one was open for 15% -> 9% of each run, Pallas kernels for 0% -> 0%
where the time goes in v1:
time: 269 us
  waiting for transfers between devices  116 us (43%)
  blocking collectives  81.4 us (30%)
  matrix products  49.9 us (19%)
  starting transfers between devices  11 us (4%)
  other arithmetic  7.79 us (3%)
    ppermute x1, waiting for transfers between devices, shards(): cotangent = lax.ppermute(cotangent, 'edp', ring)  116 us
    all_to_all x1, blocking collectives, shards(): lax.all_to_all(send_buffer, 'ep', split_axis=0, concat_axis=0, tiled=True)  81.4 us
    dot_general x1, matrix products, combine_rows(): halves = jnp.dot(spread, returned, preferred_element_type=jnp.float32)  10.3 us
    all_to_all x1, starting transfers between devices, shards(): lax.all_to_all(output.reshape(received.shape), 'ep', split_axis=0, concat...  7.36 us
    dot_general x1, matrix products, expert_mlp(): jnp.dot(hidden, w_down, preferred_element_type=jnp.float32)  7.05 us
    broadcast_in_dim x2, other arithmetic, shards(): grad_gate, grad_up, grad_down = (grad_g[None], grad_u[None], grad_d[None])  5.66 us
    dot_general x1, matrix products, expert_mlp(): up_pre = jnp.dot(row_data, w_up, preferred_element_type=jnp.float32)  5.6 us
  transfers between devices with their start and end apart: 3, of which 1 were waited for; matrix products, arithmetic and copies ran while one was open for 9% of the time, Pallas kernels for 0%

profile of v1, /device:TPU:66, one launch (start us, length us, event | category | flops | bytes accessed | tf_op | source)
XLA Modules:
  0.0 268.8 jit_solution(9033202278145268290)
XLA Ops:
  0.6 0.0 copy-start
  0.7 0.1 eq.62
  0.7 0.9 fusion.40
  1.6 0.1 fusion.22
  1.8 0.3 bitcast_compare_fusion
  2.1 2.8 %convolution_convert_fusion.1 = bf16[1536,2048]{1,0:T(8,128)(2,1)S(1)} fusion(pred[1536,128]{1,0:T(32,128)(4,1)S(1)} %bitcast_compare_fusion, bf16[128,2048]{1,0:T(8,128)(2,1)} %param.8), kind=kOutput, calls=%fused_computation.1 | convolution fusion | flops 808452096 | bytes 7012352 | tf_op jit(solution)/shard_map/dot_general | solution.py:49
  4.9 0.0 copy-start.4
  4.9 81.4 %all_to_all.10 = bf16[64,24,2048]{2,1,0:T(8,128)(2,1)S(1)} all-to-all(bf16[64,24,2048]{2,1,0:T(8,128)(2,1)S(1)} %bitcast.66), channel_id=1, replica_groups=mesh['edp'=2,'ep'=64] {'ep'}, dimensions={0} | all-to-all | bytes 12582912 | tf_op jit(solution)/shard_map/all_to_all | solution.py:86
  86.3 0.0 copy-done.4
  86.3 0.0 copy-start.6
  86.3 5.2 %fusion.16 = f32[1536,768]{1,0:T(8,128)S(1)} fusion(bf16[1536,2048]{1,0:T(8,128)(2,1)S(1)} %bitcast.68, bf16[1,2048,768]{2,1,0:T(8,128)(2,1)S(1)} %copy-done.4), kind=kOutput, calls=%fused_computation.19 | convolution fusion | flops 4831838208 | bytes 14155776 | tf_op jit(solution)/shard_map/dot_general | solution.py:8
  91.6 0.0 copy-done.6
  91.6 5.6 %multiply_convert_fusion = bf16[1536,768]{1,0:T(8,128)(2,1)S(1)} fusion(f32[1536,768]{1,0:T(8,128)S(1)} %fusion.16, bf16[1536,2048]{1,0:T(8,128)(2,1)S(1)} %bitcast.69, bf16[1,2048,768]{2,1,0:T(8,128)(2,1)S(1)} %copy-done.6), kind=kOutput, calls=%fused_computation.4 | convolution fusion | flops 4838916096 | bytes 16515072 | tf_op jit(solution)/shard_map/dot_general | solution.py:9
  97.2 0.0 copy-done
  97.2 7.0 %convolution_convert_fusion = bf16[1536,2048]{1,0:T(8,128)(2,1)} fusion(bf16[1536,768]{1,0:T(8,128)(2,1)S(1)} %multiply_convert_fusion, bf16[1,768,2048]{2,1,0:T(8,128)(2,1)S(1)} %copy-done), kind=kOutput, calls=%fused_computation | convolution fusion | flops 4834983936 | bytes 11796480 | tf_op jit(solution)/shard_map/dot_general | solution.py:11
  104.2 7.4 %all-to-all-start.1 = ((bf16[64,24,2048]{2,1,0:T(8,128)(2,1)}), bf16[64,24,2048]{2,1,0:T(8,128)(2,1)}, u32[]{:S(2)}, u32[]{:S(2)}) async-start(bf16[64,24,2048]{2,1,0:T(8,128)(2,1)} %bitcast.67), calls=%async_computation.1 | async-start | bytes 12582912 | tf_op jit(solution)/shard_map/all_to_all | solution.py:88
  111.6 3.0 %collective-permute-start = (bf16[256,2048]{1,0:T(8,128)(2,1)}, bf16[256,2048]{1,0:T(8,128)(2,1)}, u32[]{:S(2)}, u32[]{:S(2)}) collective-permute-start(bf16[256,2048]{1,0:T(8,128)(2,1)} %bitcast.72), channel_id=1, source_target_pairs={{0,64},{64,0},{1,65},{65,1},{2,66},{66,2},{3,67},{67,3},{4,68},{68... | collective-permute-start | bytes 3145736 | tf_op jit(solution)/shard_map/ppermute | solution.py:114
  114.6 0.6 collective-permute-start.1
  115.2 0.0 copy-start.7
  115.2 0.0 copy-start.8
  115.2 2.4 fusion.4
  117.6 0.0 copy-done.7
  117.6 0.1 copy-done.8
  117.7 1.0 fusion.9
  118.7 0.9 copy-done.5
  119.6 1.1 fusion.26
  120.7 0.8 convolution_convert_fusion.7
  121.5 0.0 copy-start.1
  121.5 0.0 copy-start.2
  121.5 0.0 copy-start.3
  121.5 0.7 convolution_convert_fusion.5
  122.2 0.5 copy-done.1
  122.7 0.6 convolution_convert_fusion.3
  123.3 0.0 copy-done.2
  123.3 0.0 copy-done.3
  123.4 116.2 %collective-permute-done.1 = bf16[256,2048]{1,0:T(8,128)(2,1)} collective-permute-done((bf16[256,2048]{1,0:T(8,128)(2,1)}, bf16[256,2048]{1,0:T(8,128)(2,1)}, u32[]{:S(2)}, u32[]{:S(2)}) %collective-permute-start.1) | collective-permute-done | bytes 1048608 | tf_op jit(solution)/shard_map/ppermute | solution.py:115
  239.6 2.2 fusion.2
  241.8 0.0 collective-permute-done
  241.8 2.3 fusion.25
  244.2 1.7 convolution_convert_fusion.4
  245.9 2.2 fusion.7
  248.2 1.8 convolution_convert_fusion.6
  250.0 1.9 convolution_convert_fusion.2
  251.9 3.4 %add_bitcast_fusion.1 = (f32[1,1024,768]{2,1,0:T(8,128)}, f32[1,1024,768]{2,1,0:T(8,128)}) fusion(bf16[1024,768]{1,0:T(8,128)(2,1)S(1)} %convolution_convert_fusion.4, bf16[1024,768]{1,0:T(8,128)(2,1)S(1)} %convolution_convert_fusion.5, bf16[1024,768]{1,0:T(8,128)(2,1)S(1)} %convolution_convert_fusion.6, bf16[1024,768]{1,0:T(8,128)(2,1)S(1)} %convolution_convert_fusion.7), kind=kLoop, calls=%fused_computation.22 | loop fusion | flops 4718592 | bytes 12582912 | tf_op jit(solution)/shard_map/broadcast_in_dim | solution.py:116
  255.3 2.3 add_bitcast_fusion
  257.5 0.0 all-to-all-done.1
  257.5 10.3 %fusion.18 = f32[256,2048]{1,0:T(8,128)S(1)} fusion(bf16[64,24,2048]{2,1,0:T(8,128)(2,1)} %all-to-all-done.1, s32[256,64]{0,1:T(8,128)S(1)} %pad_add_fusion, bf16[256,64]{0,1:T(8,128)(2,1)S(1)} %pad_maximum_fusion), kind=kOutput, calls=%fused_computation.26 | convolution fusion | flops 1611399168 | bytes 8486912 | tf_op jit(solution)/shard_map/dot_general | solution.py:71
  267.9 0.9 fusion.23
  (6 shorter events, 0.1 us)
Async XLA Ops:
  0.6 96.5 %copy-start = (bf16[1,768,2048]{2,1,0:T(8,128)(2,1)S(1)}, bf16[1,768,2048]{2,1,0:T(8,128)(2,1)}, u32[]{:S(2)}) copy-start(bf16[1,768,2048]{2,1,0:T(8,128)(2,1)} %param.13) | copy-start | bytes 9437188
  4.9 81.5 %copy-start.4 = (bf16[1,2048,768]{2,1,0:T(8,128)(2,1)S(1)}, bf16[1,2048,768]{2,1,0:T(8,128)(2,1)}, u32[]{:S(2)}) copy-start(bf16[1,2048,768]{2,1,0:T(8,128)(2,1)} %param.11) | copy-start | bytes 9437188
  86.3 5.2 %copy-start.6 = (bf16[1,2048,768]{2,1,0:T(8,128)(2,1)S(1)}, bf16[1,2048,768]{2,1,0:T(8,128)(2,1)}, u32[]{:S(2)}) copy-start(bf16[1,2048,768]{2,1,0:T(8,128)(2,1)} %param.12) | copy-start | bytes 9437188
  104.2 153.3 %all-to-all-start.1 = ((bf16[64,24,2048]{2,1,0:T(8,128)(2,1)}), bf16[64,24,2048]{2,1,0:T(8,128)(2,1)}, u32[]{:S(2)}, u32[]{:S(2)}) async-start(bf16[64,24,2048]{2,1,0:T(8,128)(2,1)} %bitcast.67), calls=%async_computation.1 | async-start | bytes 12582912 | tf_op jit(solution)/shard_map/all_to_all | solution.py:88
  111.6 130.2 %collective-permute-start = (bf16[256,2048]{1,0:T(8,128)(2,1)}, bf16[256,2048]{1,0:T(8,128)(2,1)}, u32[]{:S(2)}, u32[]{:S(2)}) collective-permute-start(bf16[256,2048]{1,0:T(8,128)(2,1)} %bitcast.72), channel_id=1, source_target_pairs={{0,64},{64,0},{1,65},{65,1},{2,66},{66,2},{3,67},{67,3},{4,68},{68... | collective-permute-start | bytes 3145736 | tf_op jit(solution)/shard_map/ppermute | solution.py:114
  114.6 125.0 %collective-permute-start.1 = (bf16[256,2048]{1,0:T(8,128)(2,1)}, bf16[256,2048]{1,0:T(8,128)(2,1)}, u32[]{:S(2)}, u32[]{:S(2)}) collective-permute-start(bf16[256,2048]{1,0:T(8,128)(2,1)} %bitcast.70), channel_id=1, source_target_pairs={{0,64},{64,0},{1,65},{65,1},{2,66},{66,2},{3,67},{67,3},{4,68},{68... | collective-permute-start | bytes 3145736 | tf_op jit(solution)/shard_map/ppermute | solution.py:115
  115.2 2.4 copy-start.7
  115.2 2.5 copy-start.8
  117.7 1.9 copy-start.5
  121.5 1.2 copy-start.1
  121.5 1.8 copy-start.2
  121.5 1.8 copy-start.3

commit v2 on v0

v2 whole, which is shorter than its diff:
```python
import jax
import jax.numpy as jnp
from jax import lax
from jax.experimental import pallas as pl
from jax.experimental.pallas import tpu as pltpu
from jax.sharding import Mesh, PartitionSpec as P

VMEM_LIMIT = 56 * 2**20


def expert_grads(inputs, cotangent, w_gate, w_up, w_down):
    gate_pre = jnp.dot(inputs, w_gate, preferred_element_type=jnp.float32)
    up_pre = jnp.dot(inputs, w_up, preferred_element_type=jnp.float32)
    activated = jax.nn.silu(gate_pre)
    hidden = (activated * up_pre).astype(jnp.bfloat16)
    d_hidden = jnp.einsum("rd,fd->rf", cotangent, w_down, preferred_element_type=jnp.float32)
    sigmoid_gate = jax.nn.sigmoid(gate_pre)
    d_gate = (d_hidden * up_pre * sigmoid_gate * (1.0 + gate_pre * (1.0 - sigmoid_gate))).astype(
        jnp.bfloat16
    )
    d_up = (d_hidden * activated).astype(jnp.bfloat16)
    return (hidden, d_gate, d_up)


def rounded(value):
    return lax.optimization_barrier(value.astype(jnp.bfloat16)).astype(jnp.float32)


def slot_table(named):
    tokens = named.shape[1]
    earlier = (
        lax.broadcasted_iota(jnp.int32, (tokens, tokens), 0)
        < lax.broadcasted_iota(jnp.int32, (tokens, tokens), 1)
    ).astype(jnp.bfloat16)
    before = jnp.dot(named.astype(jnp.bfloat16), earlier, preferred_element_type=jnp.float32)
    return jnp.where(named, before.astype(jnp.int32), -1)


def named_by(routes, first, experts):
    return routes.T[:, None, :] == first + jnp.arange(experts, dtype=jnp.int32)[None, :, None]


def select_rows(place, tokens, count):
    experts, rows = place.shape
    width = tokens.shape[1]
    step = 256 // count

    def kernel(place_ref, token_ref, out_ref):
        chosen = place_ref[...][:, None, :] == lax.broadcasted_iota(
            jnp.int32, (step, count, rows), 1
        )
        chosen = jnp.where(chosen, 1.0, 0.0).reshape(step * count, rows).astype(jnp.bfloat16)
        out_ref[...] = jnp.dot(
            chosen, token_ref[...], preferred_element_type=jnp.float32
        ).astype(jnp.bfloat16)

    return pl.pallas_call(
        kernel,
        grid=(experts // step,),
        in_specs=[
            pl.BlockSpec((step, rows), lambda i: (i, 0)),
            pl.BlockSpec((rows, width), lambda i: (0, 0)),
        ],
        out_specs=pl.BlockSpec((step * count, width), lambda i: (i, 0)),
        out_shape=jax.ShapeDtypeStruct((experts * count, width), jnp.bfloat16),
        cost_estimate=pl.CostEstimate(
            flops=2 * experts * count * rows * width,
            bytes_accessed=2 * (experts * count + rows) * width,
            transcendentals=0,
        ),
        compiler_params=pltpu.CompilerParams(vmem_limit_bytes=VMEM_LIMIT),
    )(place, tokens)


def expert_mlp(row_data, w_gate, w_up, w_down, out_shape, slot, slots, store, into=None):
    rows, width = row_data.shape
    hidden_size = w_gate.shape[1]
    step = 256
    steps = hidden_size // step

    def kernel(x_ref, gate_ref, up_ref, down_ref, *rest):
        out_ref, sum_ref, stage_ref, sem = rest[-4:]
        x = x_ref[...]
        gate_pre = jnp.dot(x, gate_ref[...], preferred_element_type=jnp.float32)
        up_pre = jnp.dot(x, up_ref[...], preferred_element_type=jnp.float32)
        hidden = (jax.nn.silu(gate_pre) * up_pre).astype(jnp.bfloat16)
        part = jnp.dot(hidden, down_ref[...], preferred_element_type=jnp.float32)
        at = pl.program_id(0)

        @pl.when(at == 0)
        def _():
            sum_ref[...] = part

        @pl.when((at > 0) & (at < steps - 1))
        def _():
            sum_ref[...] += part

        @pl.when(at == steps - 1)
        def _():
            store(stage_ref, sum_ref[...] + part)
            copy = pltpu.make_async_copy(stage_ref, out_ref.at[:, slot : slot + slots, :], sem)
            copy.start()
            copy.wait()

    operands = [row_data, w_gate, w_up, w_down]
    in_specs = [
        pl.BlockSpec((rows, width), lambda j: (0, 0)),
        pl.BlockSpec((width, step), lambda j: (0, j)),
        pl.BlockSpec((width, step), lambda j: (0, j)),
        pl.BlockSpec((step, width), lambda j: (j, 0)),
    ]
    aliases = {}
    if into is not None:
        operands.append(into)
        in_specs.append(pl.BlockSpec(memory_space=pl.ANY))
        aliases = {4: 0}
    return pl.pallas_call(
        kernel,
        grid=(steps,),
        in_specs=in_specs,
        out_specs=pl.BlockSpec(memory_space=pl.ANY),
        out_shape=jax.ShapeDtypeStruct(out_shape, jnp.bfloat16),
        scratch_shapes=[
            pltpu.VMEM((rows, width), jnp.float32),
            pltpu.VMEM((out_shape[0], slots, width), jnp.bfloat16),
            pltpu.SemaphoreType.DMA,
        ],
        input_output_aliases=aliases,
        cost_estimate=pl.CostEstimate(
            flops=6 * rows * width * hidden_size,
            bytes_accessed=2 * (2 * rows + 3 * hidden_size) * width,
            transcendentals=rows * hidden_size,
        ),
        compiler_params=pltpu.CompilerParams(vmem_limit_bytes=VMEM_LIMIT),
    )(*operands)


def weighted_sum(spread, returned):
    terms, rows = spread.shape
    width = returned.shape[1]
    tokens = terms // 2
    step = 512

    def kernel(spread_ref, row_ref, out_ref):
        both = jnp.dot(spread_ref[...], row_ref[...], preferred_element_type=jnp.float32)
        out_ref[...] = (both[:tokens] + both[tokens:]).astype(jnp.bfloat16)

    return pl.pallas_call(
        kernel,
        grid=(width // step,),
        in_specs=[
            pl.BlockSpec((terms, rows), lambda j: (0, 0)),
            pl.BlockSpec((rows, step), lambda j: (0, j)),
        ],
        out_specs=pl.BlockSpec((tokens, step), lambda j: (0, j)),
        out_shape=jax.ShapeDtypeStruct((tokens, width), jnp.bfloat16),
        cost_estimate=pl.CostEstimate(
            flops=2 * terms * rows * width, bytes_accessed=2 * rows * width, transcendentals=0
        ),
        compiler_params=pltpu.CompilerParams(vmem_limit_bytes=VMEM_LIMIT),
    )(spread, returned)


def exchange(value, axes):
    return lax.all_to_all(value, axes, split_axis=0, concat_axis=0, tiled=True)


def layer(tokens, routes, gate_weights, w_gate, w_up, w_down, saved_inputs, saved_cotangent):
    halves, plane = lax.axis_size("half"), lax.axis_size("plane")
    every = ("half", "plane")
    experts = halves * plane
    tok_rows, width = tokens.shape
    top_count = routes.shape[1]
    capacity = 3 * tok_rows * top_count // (2 * experts)
    early = 2 * capacity // 3
    late = capacity - early
    gate_mat, up_mat, down_mat = (w_gate[0], w_up[0], w_down[0])
    replicas = lax.axis_size("edp")
    ring = [(r, (r + 1) % replicas) for r in range(replicas)]
    swap = [(0, 1), (1, 0)]
    half = lax.axis_index("half")

    other_routes = lax.ppermute(routes, "half", swap)
    other_tokens = lax.ppermute(tokens, "half", swap)

    named = named_by(routes, 0, experts)
    slots = slot_table(jnp.any(named, axis=0))
    send1 = select_rows(slots, tokens, early)
    received1 = exchange(send1.reshape(experts, early, width), every)
    is_low = half == 0
    low_routes = jnp.where(is_low, routes, other_routes)
    high_routes = jnp.where(is_low, other_routes, routes)
    low_tokens = jnp.where(is_low, tokens, other_tokens)
    high_tokens = jnp.where(is_low, other_tokens, tokens)
    places = []
    for number, block_routes in enumerate((low_routes, high_routes)):
        place = slot_table(jnp.any(named_by(block_routes, half * plane, plane), axis=0))
        places.append(jnp.where(place >= early, place - early + number * late, -1))
    send2 = select_rows(
        jnp.concatenate(places, axis=1),
        jnp.concatenate([low_tokens, high_tokens], axis=0),
        halves * late,
    )
    received2 = exchange(send2.reshape(plane, halves * late, width), "plane")

    def store1(stage_ref, value):
        stage_ref[...] = value.reshape(experts, early, width).astype(jnp.bfloat16)

    def store2(stage_ref, value):
        value = value.reshape(plane, halves, late, width)
        for number in range(halves):
            stage_ref[number * plane : (number + 1) * plane] = value[:, number].astype(jnp.bfloat16)

    shape = (experts, capacity, width)
    output = expert_mlp(
        received1.reshape(-1, width), gate_mat, up_mat, down_mat,
        shape, 0, early, store1,
    )
    output = expert_mlp(
        received2.reshape(-1, width), gate_mat, up_mat, down_mat,
        shape, early, late, store2, into=output,
    )
    returned = exchange(output, every)

    weight = jnp.sum(jnp.where(named, gate_weights.T[:, None, :], 0.0), axis=0).T
    high = lax.reduce_precision(weight, 8, 7)
    terms = jnp.concatenate([high, weight - high], axis=0).astype(jnp.bfloat16)
    place = jnp.concatenate([slots.T, slots.T], axis=0)
    spread = jnp.where(
        place[:, :, None] == jnp.arange(capacity, dtype=jnp.int32)[None, None, :],
        terms[:, :, None],
        jnp.bfloat16(0.0),
    ).reshape(2 * tok_rows, experts * capacity)
    combined = weighted_sum(spread, returned.reshape(-1, width))

    own_index = lax.axis_index("edp")
    half_width = width // replicas
    half_hidden = gate_mat.shape[1] // replicas
    grad_g = jnp.zeros((half_width, gate_mat.shape[1]), jnp.float32)
    grad_u = jnp.zeros((half_width, gate_mat.shape[1]), jnp.float32)
    grad_d = jnp.zeros((half_hidden, width), jnp.float32)
    inputs, cotangent = saved_inputs[0], saved_cotangent[0]
    for replica in range(replicas):
        hidden, d_gate, d_up = expert_grads(inputs, cotangent, gate_mat, up_mat, down_mat)
        in_cols = lax.dynamic_slice_in_dim(inputs, own_index * half_width, half_width, 1)
        hidden_cols = lax.dynamic_slice_in_dim(hidden, own_index * half_hidden, half_hidden, 1)
        grad_g = grad_g + rounded(
            jnp.einsum("rd,rf->df", in_cols, d_gate, preferred_element_type=jnp.float32)
        )
        grad_u = grad_u + rounded(
            jnp.einsum("rd,rf->df", in_cols, d_up, preferred_element_type=jnp.float32)
        )
        grad_d = grad_d + rounded(
            jnp.einsum("rf,rd->fd", hidden_cols, cotangent, preferred_element_type=jnp.float32)
        )
        if replica + 1 < replicas:
            inputs = lax.ppermute(inputs, "edp", ring)
            cotangent = lax.ppermute(cotangent, "edp", ring)
    grad_gate, grad_up, grad_down = (grad_g[None], grad_u[None], grad_d[None])
    return (combined, grad_gate, grad_up, grad_down)


def solution(mesh):
    replicas, ep = mesh.devices.shape
    split = Mesh(mesh.devices.reshape(replicas, 2, ep // 2), ("edp", "half", "plane"))
    tok, own, rep = P(("edp", "half", "plane"), None), ("half", "plane"), "edp"
    return jax.shard_map(
        layer,
        mesh=split,
        in_specs=(tok, tok, tok, P(own), P(own), P(own), P(own, rep, None), P(own, rep, None)),
        out_specs=(tok, P(own, rep, None), P(own, rep, None), P(own, rep, None)),
        check_vma=False,
    )
```

time: 299 us -> 229 us (0.77)
  Pallas kernels: 0 us -> 41.9 us
  waiting for transfers between devices: 149 us -> 108 us
  other arithmetic: 48.9 us -> 10.7 us
  local copies, waits for them, and re-layouts: 29.1 us -> 3.58 us
  starting transfers between devices: 16.2 us -> 31.1 us
  between operations: 14.3 us -> 0.92 us
  matrix products: 36.3 us -> 29.7 us
    all_to_all x2 -> x3, waiting for transfers between devices: 146 us -> 45.5 us  [exchange(): return lax.all_to_all(value, axes, split_axis=0, concat_axis=0, tiled=True)]
    ppermute x0 -> x4, waiting for transfers between devices: none -> 62.2 us  [the longest x1 52.6 us: layer(): other_routes = lax.ppermute(routes, 'half', swap)]
    pallas_call x0 -> x5, Pallas kernels: none -> 41.9 us  [the longest x2 28.6 us: expert_mlp(): pl.pallas_call(kernel, grid=(steps,), in_specs=in_specs, out_specs=pl.Blo...]
    another operation x2 -> x1, other arithmetic: 31.1 us -> 0.01 us
    gather x1 -> x0, local copies, waits for them, and re-layouts: 12.7 us -> none  [shards(): picked = returned.reshape(experts * capacity, width)[position]]
    dot_general x9, matrix products: 27 us -> 15.8 us  [the longest x2 5.05 us: layer(): jnp.einsum('rf,rd->fd', hidden_cols, cotangent, preferred_element_type=jn...]
    scatter x1 -> x0, local copies, waits for them, and re-layouts: 10.7 us -> none  [shards(): send_buffer.at[position].set(jnp.repeat(tokens, top_count, axis=0))]
    all_to_all x2 -> x3, starting transfers between devices: 15.9 us -> 25.4 us  [exchange(): return lax.all_to_all(value, axes, split_axis=0, concat_axis=0, tiled=True)]
  transfers between devices with their start and end apart: 3 -> 7, of which waited for: 3 -> 4; matrix products, arithmetic and copies ran while one was open for 15% -> 18% of each run, Pallas kernels for 0% -> 14%
where the time goes in v2:
time: 229 us; the launch traced here: 226 us
  waiting for transfers between devices  108 us (47%)
  Pallas kernels  41.9 us (18%)
  starting transfers between devices  31.1 us (14%)
  matrix products  29.7 us (13%)
  other arithmetic  10.7 us (5%)
  local copies, waits for them, and re-layouts  3.58 us (2%)
    ppermute x1, waiting for transfers between devices, layer(): other_routes = lax.ppermute(routes, 'half', swap)  52.6 us
    all_to_all x3, waiting for transfers between devices, exchange(): return lax.all_to_all(value, axes, split_axis=0, concat_axis=0, tiled=True)  45.5 us
    pallas_call x2, Pallas kernels, expert_mlp(): pl.pallas_call(kernel, grid=(steps,), in_specs=in_specs, out_specs=pl.Blo...  28.6 us
    all_to_all x3, starting transfers between devices, exchange(): return lax.all_to_all(value, axes, split_axis=0, concat_axis=0, tiled=True)  25.4 us
    ppermute x1, waiting for transfers between devices, layer(): other_tokens = lax.ppermute(tokens, 'half', swap)  9.64 us
    pallas_call x2, Pallas kernels, select_rows(): pl.pallas_call(kernel, grid=(experts // step,), in_specs=[pl.BlockSpec((s...  7.73 us
    broadcast_in_dim x2, other arithmetic, layer(): grad_gate, grad_up, grad_down = (grad_g[None], grad_u[None], grad_d[None])  5.66 us
    pallas_call x1, Pallas kernels, weighted_sum(): pl.pallas_call(kernel, grid=(width // step,), in_specs=[pl.BlockSpec((ter...  5.6 us
  transfers between devices with their start and end apart: 7, of which 4 were waited for; matrix products, arithmetic and copies ran while one was open for 18% of the time, Pallas kernels for 14%

profile of v2, /device:TPU:66, one launch (start us, length us, event | category | flops | bytes accessed | tf_op | source)
XLA Modules:
  0.0 225.6 jit_solution(16297701029790068910)
XLA Ops:
  0.6 0.7 fusion.15
  1.4 0.8 fusion.place_ref
  2.1 4.6 %shard_map.112 = bf16[1024,2048]{1,0:T(8,128)(2,1)} custom-call(s32[64,128]{1,0:T(8,128)} %fusion.place_ref, bf16[128,2048]{1,0:T(8,128)(2,1)} %token_ref.1), custom_call_target="tpu_custom_call" | custom-call | flops 536870912 | bytes 4718592 | tf_op jit(solution)/shard_map/pallas_call | solution.py:57
  6.7 9.3 %all-to-all-start.1 = ((bf16[64,16,2048]{2,1,0:T(8,128)(2,1)}), bf16[64,16,2048]{2,1,0:T(8,128)(2,1)}, u32[]{:S(2)}, u32[]{:S(2)}) async-start(bf16[64,16,2048]{2,1,0:T(8,128)(2,1)} %bitcast.66), calls=%async_computation.1 | async-start | bytes 8388608 | tf_op jit(solution)/shard_map/all_to_all | solution.py:165
  16.0 1.8 collective-permute-start
  17.8 0.3 collective-permute-start.1
  18.2 52.6 %collective-permute-done = s32[128,8]{0,1:T(8,128)S(1)} collective-permute-done((s32[128,8]{0,1:T(8,128)S(1)}, s32[128,8]{0,1:T(8,128)S(1)}, u32[]{:S(2)}, u32[]{:S(2)}) %collective-permute-start) | collective-permute-done | bytes 4128 | tf_op jit(solution)/shard_map/ppermute | solution.py:183
  70.7 0.1 compare_reduce_fusion.1
  70.8 0.1 add_select_fusion
  71.0 0.1 add_select_fusion.1
  71.1 0.6 pad_add_fusion.1.place_ref
  71.7 9.6 %collective-permute-done.1 = bf16[128,2048]{1,0:T(8,128)(2,1)S(1)} collective-permute-done((bf16[128,2048]{1,0:T(8,128)(2,1)S(1)}, bf16[128,2048]{1,0:T(8,128)(2,1)S(1)}, u32[]{:S(2)}, u32[]{:S(2)}) %collective-permute-start.1) | collective-permute-done | bytes 524320 | tf_op jit(solution)/shard_map/ppermute | solution.py:184
  81.4 0.1 broadcast_select_fusion.1
  81.4 1.1 pad_maximum_fusion.token_ref
  82.5 3.1 %shard_map.111 = bf16[512,2048]{1,0:T(8,128)(2,1)} custom-call(s32[32,256]{1,0:T(8,128)} %pad_add_fusion.1.place_ref, bf16[256,2048]{1,0:T(8,128)(2,1)} %pad_maximum_fusion.token_ref), custom_call_target="tpu_custom_call" | custom-call | flops 536870912 | bytes 3145728 | tf_op jit(solution)/shard_map/pallas_call | solution.py:57
  85.6 5.9 %all-to-all-start = ((bf16[32,16,2048]{2,1,0:T(8,128)(2,1)}), bf16[32,16,2048]{2,1,0:T(8,128)(2,1)S(1)}, u32[]{:S(2)}, u32[]{:S(2)}) async-start(bf16[32,16,2048]{2,1,0:T(8,128)(2,1)} %bitcast.68), calls=%async_computation | async-start | bytes 4194304 | tf_op jit(solution)/shard_map/all_to_all | solution.py:165
  91.5 3.0 %collective-permute-start.2 = (bf16[256,2048]{1,0:T(8,128)(2,1)}, bf16[256,2048]{1,0:T(8,128)(2,1)}, u32[]{:S(2)}, u32[]{:S(2)}) collective-permute-start(bf16[256,2048]{1,0:T(8,128)(2,1)} %bitcast.18), channel_id=1, source_target_pairs={{0,64},{64,0},{1,65},{65,1},{2,66},{66,2},{3,67},{67,3},{4,68},{68... | collective-permute-start | bytes 3145736 | tf_op jit(solution)/shard_map/ppermute | solution.py:257
  94.5 0.6 collective-permute-start.3
  95.2 17.9 %shard_map.113.rest_0_ = bf16[64,24,2048]{2,1,0:T(8,128)(2,1)} custom-call(bf16[1024,2048]{1,0:T(8,128)(2,1)} %bitcast.14.x_ref, bf16[2048,768]{1,0:T(8,128)(2,1)} %bitcast.73, bf16[2048,768]{1,0:T(8,128)(2,1)} %bitcast.75, bf16[768,2048]{1,0:T(8,128)(2,1)} %bitcast.71), custom_call_target="tpu_custom_call" | custom-call | flops 9663676416 | bytes 17825792 | tf_op jit(solution)/shard_map/pallas_call | solution.py:117
  113.1 4.2 %all-to-all-done = bf16[32,16,2048]{2,1,0:T(8,128)(2,1)S(1)} async-done(((bf16[32,16,2048]{2,1,0:T(8,128)(2,1)}), bf16[32,16,2048]{2,1,0:T(8,128)(2,1)S(1)}, u32[]{:S(2)}, u32[]{:S(2)}) %all-to-all-start) | async-done | bytes 2097184 | tf_op jit(solution)/shard_map/all_to_all | solution.py:165
  117.2 1.3 copy-done
  118.6 10.7 %shard_map.114 = bf16[64,24,2048]{2,1,0:T(8,128)(2,1)} custom-call(bf16[512,2048]{1,0:T(8,128)(2,1)} %bitcast.67, bf16[2048,768]{1,0:T(8,128)(2,1)} %bitcast.74, bf16[2048,768]{1,0:T(8,128)(2,1)} %bitcast.76, bf16[768,2048]{1,0:T(8,128)(2,1)} %bitcast.72, bf16[64,24,2048]{2,1,0:T(8,128)(2,1)} %shard_map.113.rest_0_), custom_call_target="tpu_custom_call", output_to_operand_aliasing={{}: (4, {})} | custom-call | flops 4831838208 | bytes 13631488 | tf_op jit(solution)/shard_map/pallas_call | solution.py:117
  129.3 0.0 copy-start.2
  129.3 10.2 %all-to-all-start.2 = ((bf16[64,24,2048]{2,1,0:T(8,128)(2,1)}), bf16[64,24,2048]{2,1,0:T(8,128)(2,1)}, u32[]{:S(2)}, u32[]{:S(2)}) async-start(bf16[64,24,2048]{2,1,0:T(8,128)(2,1)} %shard_map.114), calls=%async_computation.2 | async-start | bytes 12582912 | tf_op jit(solution)/shard_map/all_to_all | solution.py:165
  139.6 2.4 %fusion.30 = f32[256,768]{1,0:T(8,128)S(1)} fusion(bf16[1,256,2048]{2,1,0:T(8,128)(2,1)} %param.15, bf16[1,768,2048]{2,1,0:T(8,128)(2,1)S(1)} %copy-done.2), kind=kOutput, calls=%fused_computation.67 | convolution fusion | flops 805306368 | bytes 4980736 | tf_op jit(solution)/shard_map/rd,fd->rf/dot_general | solution.py:16
  142.0 2.3 %fusion.4 = (f32[256,768]{1,0:T(8,128)S(1)}, f32[256,768]{1,0:T(8,128)S(1)}) fusion(bf16[1,2048,768]{2,1,0:T(8,128)(2,1)S(1)} %copy-done.4, bf16[1,256,2048]{2,1,0:T(8,128)(2,1)} %param.14), kind=kOutput, calls=%fused_computation.24 | convolution fusion | flops 806092800 | bytes 5767168 | tf_op jit(solution)/shard_map/dot_general | solution.py:12
  144.3 3.0 %convolution_convert_fusion.3 = bf16[1024,768]{1,0:T(8,128)(2,1)} fusion(bf16[1,256,2048]{2,1,0:T(8,128)(2,1)} %param.14, s32[]{:T(128)S(6)} %select_n.74, f32[256,768]{1,0:T(8,128)S(1)} %fusion.30, f32[256,768]{1,0:T(8,128)S(1)} %get-tuple-element.15), kind=kOutput, calls=%fused_computation.6 | convolution fusion | flops 404619264 | bytes 3670020 | tf_op jit(solution)/shard_map/rd,rf->df/dot_general | solution.py:251
  147.3 2.2 fusion.27
  149.6 3.0 %convolution_convert_fusion.5 = bf16[1024,768]{1,0:T(8,128)(2,1)} fusion(bf16[1,256,2048]{2,1,0:T(8,128)(2,1)} %param.14, s32[]{:T(128)S(6)} %select_n.74, f32[256,768]{1,0:T(8,128)S(1)} %get-tuple-element.15, f32[256,768]{1,0:T(8,128)S(1)} %fusion.30, f32[256,768]{1,0:T(8,128)S(1)} %fusion.27), kind=kOutput, calls=%fused_computation.8 | convolution fusion | flops 405405696 | bytes 4456452 | tf_op jit(solution)/shard_map/rd,rf->df/dot_general | solution.py:248
  152.6 3.1 %convolution_convert_fusion.1 = bf16[384,2048]{1,0:T(8,128)(2,1)} fusion(f32[256,768]{1,0:T(8,128)S(1)} %fusion.27, s32[]{:T(128)S(6)} %select_n.75, f32[256,768]{1,0:T(8,128)S(1)} %get-tuple-element.14, bf16[1,256,2048]{2,1,0:T(8,128)(2,1)} %param.15), kind=kOutput, calls=%fused_computation.4 | convolution fusion | flops 403636224 | bytes 3407876 | tf_op jit(solution)/shard_map/rf,rd->fd/dot_general | solution.py:254
  155.6 0.1 broadcast_in_dim.59
  155.7 1.2 copy.17
  156.9 0.1 eq.63
  157.0 0.5 copy.16
  157.5 0.1 eq.66
  157.6 2.4 %compare_select_fusion.spread_ref = bf16[256,1536]{1,0:T(8,128)(2,1)} fusion(bf16[256,1536]{1,0:T(8,128)(2,1)} %copy.17, s32[256,1536]{1,0:T(8,128)S(1)} %copy.16, s32[1536]{0:T(1024)S(1)} %eq.66), kind=kLoop, calls=%fused_computation.9 | loop fusion | flops 786432 | bytes 3151872 | tf_op jit(solution)/shard_map/jit(_where)/select_n | solution.py:229
  159.9 2.4 %fusion.32 = f32[256,768]{1,0:T(8,128)S(1)} fusion(bf16[256,2048]{1,0:T(8,128)(2,1)} %collective-permute-done.3, bf16[1,768,2048]{2,1,0:T(8,128)(2,1)S(1)} %copy-done.3), kind=kOutput, calls=%fused_computation.69 | convolution fusion | flops 805306368 | bytes 4980736 | tf_op jit(solution)/shard_map/rd,fd->rf/dot_general | solution.py:16
  162.4 2.3 %fusion.3 = (f32[256,768]{1,0:T(8,128)S(1)}, f32[256,768]{1,0:T(8,128)S(1)}) fusion(bf16[256,2048]{1,0:T(8,128)(2,1)} %collective-permute-done.2, bf16[1,2048,768]{2,1,0:T(8,128)(2,1)S(1)} %copy-done.5), kind=kOutput, calls=%fused_computation.21 | convolution fusion | flops 806092800 | bytes 5767168 | tf_op jit(solution)/shard_map/dot_general | solution.py:12
  164.7 1.9 convolution_convert_fusion.2
  166.6 0.2 copy-done.7
  166.8 2.2 fusion.35
  169.0 1.8 convolution_convert_fusion.4
  170.8 2.0 convolution_convert_fusion
  172.8 0.2 copy-done.10
  173.0 3.4 %add_bitcast_fusion.1 = (f32[1,1024,768]{2,1,0:T(8,128)}, f32[1,1024,768]{2,1,0:T(8,128)}) fusion(bf16[1024,768]{1,0:T(8,128)(2,1)S(1)} %convolution_convert_fusion.2, bf16[1024,768]{1,0:T(8,128)(2,1)S(1)} %copy-done.9, bf16[1024,768]{1,0:T(8,128)(2,1)S(1)} %convolution_convert_fusion.4, bf16[1024,768]{1,0:T(8,128)(2,1)S(1)} %copy-done.10), kind=kLoop, calls=%fused_computation.1 | loop fusion | flops 4718592 | bytes 12582912 | tf_op jit(solution)/shard_map/broadcast_in_dim | solution.py:259
  176.4 2.3 %add_bitcast_fusion = f32[1,384,2048]{2,1,0:T(8,128)} fusion(bf16[384,2048]{1,0:T(8,128)(2,1)S(1)} %convolution_convert_fusion, bf16[384,2048]{1,0:T(8,128)(2,1)S(1)} %copy-done.1), kind=kLoop, calls=%fused_computation | loop fusion | flops 2359296 | bytes 6291456 | tf_op jit(solution)/shard_map/broadcast_in_dim | solution.py:259
  178.7 41.3 %all-to-all-done.2 = bf16[64,24,2048]{2,1,0:T(8,128)(2,1)} async-done(((bf16[64,24,2048]{2,1,0:T(8,128)(2,1)}), bf16[64,24,2048]{2,1,0:T(8,128)(2,1)}, u32[]{:S(2)}, u32[]{:S(2)}) %all-to-all-start.2) | async-done | bytes 6291488 | tf_op jit(solution)/shard_map/all_to_all | solution.py:165
  220.0 5.6 %shard_map.115 = bf16[128,2048]{1,0:T(8,128)(2,1)} custom-call(bf16[256,1536]{1,0:T(8,128)(2,1)} %compare_select_fusion.spread_ref, bf16[1536,2048]{1,0:T(8,128)(2,1)} %bitcast.15.row_ref), custom_call_target="tpu_custom_call" | custom-call | flops 1610612736 | bytes 6291456 | tf_op jit(solution)/shard_map/pallas_call | solution.py:148
  (34 shorter events, 0.1 us)
Async XLA Ops:
  6.7 9.3 %copy-start.12 = (s32[128,8]{0,1:T(8,128)S(1)}, s32[128,8]{0,1:T(8,128)}, u32[]{:S(2)}) copy-start(s32[128,8]{0,1:T(8,128)} %param.9) | copy-start | bytes 12292
  6.7 11.1 %copy-start.8 = (bf16[128,2048]{1,0:T(8,128)(2,1)S(1)}, bf16[128,2048]{1,0:T(8,128)(2,1)}, u32[]{:S(2)}) copy-start(bf16[128,2048]{1,0:T(8,128)(2,1)} %token_ref.1) | copy-start | bytes 1572868
  6.7 78.9 %all-to-all-start.1 = ((bf16[64,16,2048]{2,1,0:T(8,128)(2,1)}), bf16[64,16,2048]{2,1,0:T(8,128)(2,1)}, u32[]{:S(2)}, u32[]{:S(2)}) async-start(bf16[64,16,2048]{2,1,0:T(8,128)(2,1)} %bitcast.66), calls=%async_computation.1 | async-start | bytes 8388608 | tf_op jit(solution)/shard_map/all_to_all | solution.py:165
  16.0 54.7 %collective-permute-start = (s32[128,8]{0,1:T(8,128)S(1)}, s32[128,8]{0,1:T(8,128)S(1)}, u32[]{:S(2)}, u32[]{:S(2)}) collective-permute-start(s32[128,8]{0,1:T(8,128)S(1)} %copy-done.12), channel_id=1, source_target_pairs={{0,32},{32,0},{1,33},{33,1},{2,34},{34,2},{3,35},{35,3},{4,36},{36... | collective-permute-start | bytes 12296 | tf_op jit(solution)/shard_map/ppermute | solution.py:183
  17.8 63.6 %collective-permute-start.1 = (bf16[128,2048]{1,0:T(8,128)(2,1)S(1)}, bf16[128,2048]{1,0:T(8,128)(2,1)S(1)}, u32[]{:S(2)}, u32[]{:S(2)}) collective-permute-start(bf16[128,2048]{1,0:T(8,128)(2,1)S(1)} %copy-done.8), channel_id=1, source_target_pairs={{0,32},{32,0},{1,33},{33,1},{2,34},{34,2},{3,35},{35,3},{4,36},{36... | collective-permute-start | bytes 1572872 | tf_op jit(solution)/shard_map/ppermute | solution.py:184
  82.5 12.6 %copy-start.13 = (f32[128,8]{0,1:T(8,128)S(1)}, f32[128,8]{0,1:T(8,128)}, u32[]{:S(2)}) copy-start(f32[128,8]{0,1:T(8,128)} %param.10) | copy-start | bytes 12292
  85.6 31.6 %all-to-all-start = ((bf16[32,16,2048]{2,1,0:T(8,128)(2,1)}), bf16[32,16,2048]{2,1,0:T(8,128)(2,1)S(1)}, u32[]{:S(2)}, u32[]{:S(2)}) async-start(bf16[32,16,2048]{2,1,0:T(8,128)(2,1)} %bitcast.68), calls=%async_computation | async-start | bytes 4194304 | tf_op jit(solution)/shard_map/all_to_all | solution.py:165
  91.5 70.8 %collective-permute-start.2 = (bf16[256,2048]{1,0:T(8,128)(2,1)}, bf16[256,2048]{1,0:T(8,128)(2,1)}, u32[]{:S(2)}, u32[]{:S(2)}) collective-permute-start(bf16[256,2048]{1,0:T(8,128)(2,1)} %bitcast.18), channel_id=1, source_target_pairs={{0,64},{64,0},{1,65},{65,1},{2,66},{66,2},{3,67},{67,3},{4,68},{68... | collective-permute-start | bytes 3145736 | tf_op jit(solution)/shard_map/ppermute | solution.py:257
  94.5 65.4 %collective-permute-start.3 = (bf16[256,2048]{1,0:T(8,128)(2,1)}, bf16[256,2048]{1,0:T(8,128)(2,1)}, u32[]{:S(2)}, u32[]{:S(2)}) collective-permute-start(bf16[256,2048]{1,0:T(8,128)(2,1)} %bitcast.17), channel_id=1, source_target_pairs={{0,64},{64,0},{1,65},{65,1},{2,66},{66,2},{3,67},{67,3},{4,68},{68... | collective-permute-start | bytes 3145736 | tf_op jit(solution)/shard_map/ppermute | solution.py:258
  117.2 1.3 copy-start
  129.3 10.3 %copy-start.2 = (bf16[1,768,2048]{2,1,0:T(8,128)(2,1)S(1)}, bf16[1,768,2048]{2,1,0:T(8,128)(2,1)}, u32[]{:S(2)}) copy-start(bf16[1,768,2048]{2,1,0:T(8,128)(2,1)} %param.13) | copy-start | bytes 9437188
  129.3 90.7 %all-to-all-start.2 = ((bf16[64,24,2048]{2,1,0:T(8,128)(2,1)}), bf16[64,24,2048]{2,1,0:T(8,128)(2,1)}, u32[]{:S(2)}, u32[]{:S(2)}) async-start(bf16[64,24,2048]{2,1,0:T(8,128)(2,1)} %shard_map.114), calls=%async_computation.2 | async-start | bytes 12582912 | tf_op jit(solution)/shard_map/all_to_all | solution.py:165
  139.5 2.4 %copy-start.4 = (bf16[1,2048,768]{2,1,0:T(8,128)(2,1)S(1)}, bf16[1,2048,768]{2,1,0:T(8,128)(2,1)}, u32[]{:S(2)}) copy-start(bf16[1,2048,768]{2,1,0:T(8,128)(2,1)} %param.11) | copy-start | bytes 9437188
  144.3 3.0 %copy-start.6 = (bf16[1,2048,768]{2,1,0:T(8,128)(2,1)S(1)}, bf16[1,2048,768]{2,1,0:T(8,128)(2,1)}, u32[]{:S(2)}) copy-start(bf16[1,2048,768]{2,1,0:T(8,128)(2,1)} %param.12) | copy-start | bytes 9437188
  152.6 4.3 %copy-start.11 = (s32[64,128]{1,0:T(8,128)S(1)}, s32[64,128]{1,0:T(8,128)}, u32[]{:S(2)}) copy-start(s32[64,128]{1,0:T(8,128)} %fusion.place_ref) | copy-start | bytes 98308
  157.6 2.4 %copy-start.3 = (bf16[1,768,2048]{2,1,0:T(8,128)(2,1)S(1)}, bf16[1,768,2048]{2,1,0:T(8,128)(2,1)}, u32[]{:S(2)}) copy-start(bf16[1,768,2048]{2,1,0:T(8,128)(2,1)} %param.13) | copy-start | bytes 9437188
  159.9 2.4 %copy-start.5 = (bf16[1,2048,768]{2,1,0:T(8,128)(2,1)S(1)}, bf16[1,2048,768]{2,1,0:T(8,128)(2,1)}, u32[]{:S(2)}) copy-start(bf16[1,2048,768]{2,1,0:T(8,128)(2,1)} %param.11) | copy-start | bytes 9437188
  164.7 2.0 copy-start.7
  170.8 2.0 copy-start.9
  170.8 2.2 copy-start.10
  173.0 3.4 %copy-start.1 = (bf16[384,2048]{1,0:T(8,128)(2,1)S(1)}, bf16[384,2048]{1,0:T(8,128)(2,1)}, u32[]{:S(2)}) copy-start(bf16[384,2048]{1,0:T(8,128)(2,1)} %convolution_convert_fusion.1) | copy-start | bytes 4718596
